TPU v7x, 128 devices: a whole 4x4x4 slice. The times are simulated.
128 devices in a mesh: grp: 8 (over y, core), mem: 16 (over x, z).
Axes of the slice: x: 4, y: 4, z: 4, core: 2. Of those that a mesh axis runs over, the one named last changes fastest.
Arguments:
- factors: bfloat16 [256, 288, 1792], P(('grp', 'mem')), may hold values from -3 to 3
- screen: int32 [128, 18], P(('grp', 'mem')), may hold values from 0 to 1, as said below
Outputs:
- exchange_matrix: float32 [1792, 1792], P(('grp', 'mem'))
Inputs may be any that keep to these rules, and one draw needn't show every extreme that they name: screen[b, j] is 1 where auxiliary block b and occupied block j survive screening; every auxiliary block keeps at least one occupied block.
All inputs are finite; a program needn't handle non-finite values.
Results may differ from a plain program's by a relative error of at most 0.0003.
Values may be sent and summed in bfloat16 or wider, within the bound.
A program may use at most 128 MiB of HBM per device.

v0:
```python
import functools

import jax
import jax.numpy as jnp
from jax import lax
from jax.experimental import pallas as pl
from jax.experimental.pallas import tpu as pltpu
from jax.sharding import PartitionSpec as P

LANES = 128
TOP = 32767.0
MESH = pl.DeviceIdType.MESH


def bits_of(size):
    return size.bit_length() - 1


def orders_for(groups, members):
    near = [("mem", 1)]
    rows = [("grp", 2 << k) for k in range(bits_of(groups) - 1)]
    far = [("mem", 2 << k) for k in range(bits_of(members) - 1)]
    return near + rows + far, rows + near + far, far + near + rows


def kernel(
    groups, members, plan, chunks, width, x_ref, screen_ref, out_ref,
    both, turned, total, sent, got, sent_top, got_top, last,
    pair_send, pair_recv, data_send, data_recv, top_send, top_recv, end_send, end_recv,
):
    depth, basis = x_ref.shape
    own_rows = out_ref.shape[0]
    half = basis // 2
    occ_blocks = screen_ref.shape[1]
    grp, mem = lax.axis_index("grp"), lax.axis_index("mem")
    core = lax.rem(grp, 2)
    place = {"grp": grp, "mem": mem}
    levels = len(plan[0])
    starts = [0]
    for level in range(levels):
        starts.append(starts[-1] + (1 << (levels - 1 - level)))

    def peer(axis, step):
        bit = lax.rem(place[axis] // step, 2)
        there = place[axis] + (1 - 2 * bit) * step
        return (there, mem) if axis == "grp" else (grp, there)

    partner = peer("grp", 1)
    barrier = pltpu.get_barrier_semaphore()
    peers = [partner] + [peer(axis, step) for axis, step in plan[0]]
    for other in peers:
        pl.semaphore_signal(barrier, inc=1, device_id=other, device_id_type=MESH)


    def mask(j, carry):
        at = pl.ds(pl.multiple_of(j * width, width), width)
        keep = screen_ref[0, lax.rem(j, occ_blocks)].astype(jnp.float32)
        both[at, :] = (x_ref[at, :].astype(jnp.float32) * keep).astype(both.dtype)
        return carry

    pieces = 2
    piece = depth // pieces
    pair = []
    for n in range(pieces):
        lax.fori_loop(n * piece // width, (n + 1) * piece // width, mask, 0)
        if n == 0:
            pl.semaphore_wait(barrier, len(peers))
        pair.append(
            pltpu.make_async_remote_copy(
                src_ref=both.at[pl.ds(n * piece, piece)],
                dst_ref=both.at[pl.ds(depth + n * piece, piece)],
                send_sem=pair_send.at[n], recv_sem=pair_recv.at[n],
                device_id=partner, device_id_type=MESH,
            )
        )
        pair[-1].start()

    def turn(low, high):
        def one(m, carry):
            at = pl.ds(pl.multiple_of(m * 256, 256), 256)
            for k in range(low, high, LANES):
                turned[at, k : k + LANES] = both[k : k + LANES, at].T
            return carry

        lax.fori_loop(0, basis // 256, one, 0)

    early = depth // LANES * LANES
    turn(0, early)
    for copy in pair:
        copy.wait_recv()
    turn(early, 2 * depth)

    def rows_at(order, index):
        at = {"grp": grp - core, "mem": mem}
        for t, (axis, step) in enumerate(order):
            flip = index // (1 << (levels - 1 - t)) % 2
            bit = lax.rem(place[axis] // step, 2)
            at[axis] = at[axis] + flip * (1 - 2 * bit) * step
        first = (at["grp"] * members + at["mem"]) * own_rows
        second = first + members * own_rows
        return [pl.ds(pl.multiple_of(r, 8), own_rows) for r in (first, second)]

    def repeat(low, high, body):
        count = high - low
        by = 4 if count % 4 == 0 else count

        def step(t, carry):
            for u in range(by):
                body(low + t * by + u)
            return carry

        if count == by:
            step(0, 0)
        else:
            lax.fori_loop(0, count // by, step, 0)

    def columns(p):
        return slice(p * LANES, (p + 1) * LANES)

    def current(p, index, order):
        return jnp.concatenate([total[r, columns(p)] for r in rows_at(order, index)], axis=0)

    def arrived(p, level, index):
        top = got_top[p, level, pl.ds(index, 1), :]
        return got[p, starts[level] + index].astype(jnp.int32).astype(jnp.float32) * (top * (1.0 / TOP))

    def send(p, level):
        order = plan[p]
        count = 1 << (levels - 1 - level)

        def pack(i):
            value = current(p, count + i, order)
            if level:
                value = value + arrived(p, level - 1, count + i)
            top = jnp.max(jnp.abs(value), axis=0, keepdims=True)
            scale = TOP / jnp.maximum(top, 2e-34)
            sent[p, starts[level] + i] = jnp.round(value * scale).astype(jnp.int32).astype(jnp.int16)
            sent_top[p, level, pl.ds(i, 1), :] = top

        repeat(0, count, pack)
        to = peer(*order[level])
        run = pl.ds(starts[level], count)
        for here, there, a, b in (
            (sent.at[p, run], got.at[p, run], data_send, data_recv),
            (sent_top.at[p, level], got_top.at[p, level], top_send, top_recv),
        ):
            pltpu.make_async_remote_copy(
                src_ref=here, dst_ref=there, send_sem=a.at[p, level], recv_sem=b.at[p, level],
                device_id=to, device_id_type=MESH,
            ).start()

    def wait(p, level, done):
        run = pl.ds(starts[level], 1 << (levels - 1 - level))
        to = peer(*plan[p][level])
        for here, there, a, b in (
            (sent.at[p, run], got.at[p, run], data_send, data_recv),
            (sent_top.at[p, level], got_top.at[p, level], top_send, top_recv),
        ):
            copy = pltpu.make_async_remote_copy(
                src_ref=here, dst_ref=there, send_sem=a.at[p, level], recv_sem=b.at[p, level],
                device_id=to, device_id_type=MESH,
            )
            copy.wait_send() if done else copy.wait_recv()

    def keep(p, level):
        order = plan[p]

        def add(i):
            value = arrived(p, level, i)
            for n, r in enumerate(rows_at(order, i)):
                total[r, columns(p)] += value[n * own_rows : (n + 1) * own_rows]

        count = 1 << (levels - 1 - level)
        repeat(0, max(1, count // 2), add)

    parts = len(plan)
    part = 0
    for low, high in chunks:
        def multiply(m, carry):
            tall = basis // 2
            at = pl.ds(pl.multiple_of(m * tall, LANES), tall)
            total[at, low:high] = jnp.dot(
                turned[at, :],
                both[:, pl.ds(pl.multiple_of(core * half + low, LANES), high - low)],
                preferred_element_type=jnp.float32,
            )
            return carry

        lax.fori_loop(0, 2, multiply, 0)
        while part < high // LANES:
            send(part, 0)
            part += 1

    mine = pl.ds(pl.multiple_of((grp * members + mem) * own_rows, 8), own_rows)
    theirs = pl.ds(pl.multiple_of((partner[0] * members + mem) * own_rows, 8), own_rows)
    ends = []
    for level in range(levels):
        for p in range(parts):
            wait(p, level, False)
            if level + 1 < levels:
                send(p, level + 1)
            keep(p, level)
            if level + 1 == levels:
                at = pl.ds(pl.multiple_of(core * half + p * LANES, LANES), LANES)
                last[p] = total[theirs, columns(p)]
                copy = pltpu.make_async_remote_copy(
                    src_ref=last.at[p], dst_ref=out_ref.at[:, at],
                    send_sem=end_send.at[p], recv_sem=end_recv.at[p],
                    device_id=partner, device_id_type=MESH,
                )
                copy.start()
                ends.append(copy)
                out_ref[:, at] = total[mine, columns(p)]
    for copy in pair:
        copy.wait_send()
    for level in range(levels):
        for p in range(parts):
            wait(p, level, True)
    for copy in ends:
        copy.wait()


def solution(mesh):
    groups, members = mesh.shape["grp"], mesh.shape["mem"]

    def on_device(factors, screen):
        aux_rows, occ_count, basis = factors.shape
        depth = aux_rows * occ_count
        devices = groups * members
        real_rows = basis // devices
        own_rows = (real_rows + 7) // 8 * 8
        rows = factors.reshape(depth, basis)
        if own_rows != real_rows:
            rows = rows.reshape(depth, devices, real_rows)
            rows = jnp.pad(rows, ((0, 0), (0, 0), (0, own_rows - real_rows)))
            basis = devices * own_rows
            rows = rows.reshape(depth, basis)
        half = basis // 2
        parts = half // LANES
        first, second, third = orders_for(groups, members)
        plan = [(first, second, third, first, second, first, second)[p % 7] for p in range(parts)]
        chunks = [(low, min(low + 2 * LANES, half)) for low in range(0, half, 2 * LANES)]
        chips = groups * members // 2
        levels = bits_of(chips)
        block = 2 * own_rows
        places = max(8, chips // 2)
        dma = pltpu.SemaphoreType.DMA
        vmem = pl.BlockSpec(memory_space=pltpu.VMEM)
        result = pl.pallas_call(
            functools.partial(kernel, groups, members, plan, chunks, occ_count // screen.shape[1]),
            out_shape=jax.ShapeDtypeStruct((own_rows, basis), jnp.float32),
            in_specs=[vmem, pl.BlockSpec(memory_space=pltpu.SMEM)],
            out_specs=vmem,
            scratch_shapes=[
                pltpu.VMEM((2 * depth, basis), jnp.bfloat16),
                pltpu.VMEM((basis, 2 * depth), jnp.bfloat16),
                pltpu.VMEM((basis, half), jnp.float32),
                pltpu.VMEM((parts, chips - 1, block, LANES), jnp.int16),
                pltpu.VMEM((parts, chips - 1, block, LANES), jnp.int16),
                pltpu.VMEM((parts, levels, places, LANES), jnp.float32),
                pltpu.VMEM((parts, levels, places, LANES), jnp.float32),
                pltpu.VMEM((parts, own_rows, LANES), jnp.float32),
                dma((2,)), dma((2,)),
                dma((parts, levels)), dma((parts, levels)),
                dma((parts, levels)), dma((parts, levels)),
                dma((parts,)), dma((parts,)),
            ],
            compiler_params=pltpu.CompilerParams(
                collective_id=0, has_side_effects=True, vmem_limit_bytes=60 * 1024 * 1024
            ),
        )(rows, screen)
        if own_rows != real_rows:
            result = result[:real_rows].reshape(real_rows, devices, own_rows)[:, :, :real_rows]
            result = result.reshape(real_rows, devices * real_rows)
        return result

    placed = (P(("grp", "mem"), None, None), P(("grp", "mem"), None))
    return jax.shard_map(
        on_device, mesh=mesh, in_specs=placed, out_specs=P(("grp", "mem"), None), check_vma=False
    )
```

profile of v0, /device:TPU:1, one launch (start us, length us, event | category | flops | bytes accessed | tf_op | source)
XLA Modules:
  0.0 105.9 jit_solution(8653599492427916533)
XLA Ops:
  0.0 8.2 %copy.3 = bf16[2,288,1792]{1,0,2:T(2,128)(2,1)S(1)} copy(bf16[2,288,1792]{2,1,0:T(8,128)(2,1)} %param.2) | data formatting | bytes 4128768 | tf_op args[0]
  8.2 3.7 %reshape_reshape.3 = bf16[576,128,14]{0,2,1:T(8,128)(2,1)} reshape(bf16[2,288,1792]{1,0,2:T(2,128)(2,1)S(1)} %copy.3) | data formatting | bytes 4128768 | tf_op jit(solution)/shard_map/reshape;reshape | solution.py:234
  11.9 2.1 %pad.4 = bf16[576,128,16]{0,2,1:T(8,128)(2,1)S(1)} pad(bf16[576,128,14]{0,2,1:T(8,128)(2,1)} %reshape_reshape.3, bf16[]{:T(256)} %constant.2.clone.1), padding=0_0x0_0x0_2 | pad | bytes 4423682 | tf_op jit(solution)/shard_map/jit(_pad)/pad | solution.py:235
  14.0 2.7 %copy.4.x_ref = bf16[576,2048]{1,0:T(8,128)(2,1)} copy(bf16[576,2048]{0,1:T(8,128)(2,1)S(1)} %bitcast.5) | data formatting | bytes 4718592 | tf_op jit(solution)/shard_map/reshape | solution.py:237
  16.6 86.9 %shard_map.28 = f32[16,2048]{1,0:T(8,128)} custom-call(bf16[576,2048]{1,0:T(8,128)(2,1)} %copy.4.x_ref, s32[1,18]{1,0:T(1,128)} %screen_ref.1), custom_call_target="tpu_custom_call" | custom-call | tf_op jit(solution)/shard_map/pallas_call | solution.py:249
  103.5 1.2 %reshape.10 = f32[14,128,16]{2,1,0:T(8,128)S(1)} reshape(f32[14,2048]{1,0:T(8,128)} %bitcast.7) | data formatting | bytes 229376 | tf_op jit(solution)/shard_map/reshape | solution.py:273
  104.7 1.1 %reshape.11 = f32[14,1792]{1,0:T(8,128)} reshape(f32[14,128,14]{2,1,0:T(8,128)S(1)} %bitcast.6) | data formatting | bytes 200704 | tf_op jit(solution)/shard_map/reshape | solution.py:274
where the time goes:
time: 106 us
  Pallas kernels  86.9 us (82%)
  local copies, waits for them, and re-layouts  19 us (18%)
    pallas_call x1, Pallas kernels, on_device(): pl.pallas_call(functools.partial(kernel, groups, members, plan, chunks, o...  86.9 us
    unnamed x1, local copies, waits for them, and re-layouts  8.16 us
    another operation x1, local copies, waits for them, and re-layouts, on_device(): rows = rows.reshape(depth, devices, real_rows)  3.73 us
    reshape x1, local copies, waits for them, and re-layouts, on_device(): rows = rows.reshape(depth, basis)  2.67 us

commit v1 on v0

v1 whole, which is shorter than its diff:
```python
import functools

import jax
import jax.numpy as jnp
from jax import lax
from jax.experimental import pallas as pl
from jax.experimental.pallas import tpu as pltpu
from jax.sharding import PartitionSpec as P

LANES = 128
TOP = 32767.0
SIDE = 4
HEAD = 16
MESH = pl.DeviceIdType.MESH
ORDERS = ("yxz", "zxy", "xyz", "yxz", "zxy", "xyz", "yxz")


def kernel(
    members, width, orders, pieces,
    x_ref, screen_ref, out_ref,
    both, turned, total, first_sum, second_sum,
    out_one, in_one, out_two, in_two, out_three, in_three, out_four, in_four,
    load_sem, pair_send, pair_recv, one_send, one_recv, two_send, two_recv,
    three_send, three_recv, four_send, four_recv,
):
    depth, basis = x_ref.shape
    own = out_ref.shape[0]
    half = basis // 2
    parts = len(orders)
    occ_blocks = screen_ref.shape[1]
    grp, mem = lax.axis_index("grp"), lax.axis_index("mem")
    at = {"y": lax.div(grp, 2), "c": lax.rem(grp, 2), "x": lax.div(mem, SIDE), "z": lax.rem(mem, SIDE)}
    core = at["c"]

    def place(axis, d):
        return lax.rem(at[axis] + d, SIDE)

    def device(axis, d, flip=0):
        there = dict(at)
        if d:
            there[axis] = place(axis, d)
        if flip:
            there["c"] = 1 - core
        return (there["y"] * 2 + there["c"], there["x"] * SIDE + there["z"])

    last_axes = sorted({order[2] for order in orders})
    peers = [device("x", 0, 1)]
    for axis in "xyz":
        for d in range(1, SIDE):
            peers.append(device(axis, d))
            if axis in last_axes:
                peers.append(device(axis, d, 1))
    barrier = pltpu.get_barrier_semaphore()
    for other in peers:
        pl.semaphore_signal(barrier, inc=1, device_id=other, device_id_type=MESH)

    piece = depth // pieces
    loads = []
    for n in range(pieces):
        rows = pl.ds(n * piece, piece)
        loads.append(pltpu.make_async_copy(x_ref.at[rows], both.at[rows], load_sem.at[n]))
        loads[-1].start()

    total_rows = total.shape[1]
    for p in range(parts):
        total[p, basis:total_rows, :] = jnp.zeros((total_rows - basis, LANES), jnp.float32)
        tail = second_sum.shape[1]
        second_sum[p, tail - 16 : tail, :] = jnp.zeros((16, LANES), jnp.float32)

    def mask(j, carry):
        rows = pl.ds(pl.multiple_of(j * width, width), width)
        keep = screen_ref[0, lax.rem(j, occ_blocks)].astype(jnp.float32)
        both[rows, :] = (both[rows, :].astype(jnp.float32) * keep).astype(both.dtype)
        return carry

    pair = []
    partner = device("x", 0, 1)
    for n in range(pieces):
        loads[n].wait()
        lax.fori_loop(n * piece // width, (n + 1) * piece // width, mask, 0)
        if n == 0:
            pl.semaphore_wait(barrier, len(peers))
        pair.append(
            pltpu.make_async_remote_copy(
                src_ref=both.at[pl.ds(n * piece, piece)],
                dst_ref=both.at[pl.ds(depth + n * piece, piece)],
                send_sem=pair_send.at[n], recv_sem=pair_recv.at[n],
                device_id=partner, device_id_type=MESH,
            )
        )
        pair[-1].start()

    def turn(low, high):
        def one(m, carry):
            rows = pl.ds(pl.multiple_of(m * 256, 256), 256)
            for k in range(low, high, LANES):
                turned[rows, k : k + LANES] = both[k : k + LANES, rows].T
            return carry

        lax.fori_loop(0, basis // 256, one, 0)

    def multiply(tiles, low, high, fresh):
        tall = basis // 2
        columns = pl.ds(pl.multiple_of(core * half + tiles[0] * LANES, LANES), len(tiles) * LANES)

        def one(m, carry):
            rows = pl.ds(pl.multiple_of(m * tall, LANES), tall)
            value = jnp.dot(turned[rows, low:high], both[low:high, columns], preferred_element_type=jnp.float32)
            for n, p in enumerate(tiles):
                mine = value[:, n * LANES : (n + 1) * LANES]
                total[p, rows, :] = mine if fresh else total[p, rows, :] + mine
            return carry

        lax.fori_loop(0, 2, one, 0)

    def exponent(top):
        return jnp.floor(jnp.log(jnp.maximum(top, 1e-33)) * 1.4426950408889634) + 1.0

    def coded(value, power):
        return jnp.round(value * (jnp.exp2(-power) * TOP)).astype(jnp.int32).astype(jnp.int16)

    def put(ref, values):
        rows = lax.broadcasted_iota(jnp.int32, (HEAD, LANES), 0)
        head = jnp.zeros((HEAD, LANES), jnp.float32)
        for g, value in enumerate(values):
            power = exponent(jnp.max(jnp.abs(value), axis=0, keepdims=True))
            n = value.shape[0]
            ref[HEAD + g * n : HEAD + (g + 1) * n, :] = coded(value, power)
            head = jnp.where(rows == g, power, head)
        ref[0:HEAD, :] = head.astype(jnp.int32).astype(jnp.int16)

    def powers(ref):
        return jnp.exp2(ref[0:HEAD, :].astype(jnp.int32).astype(jnp.float32)) * (1.0 / TOP)

    def get(ref, scale, g, n):
        return ref[HEAD + g * n : HEAD + (g + 1) * n, :].astype(jnp.int32).astype(jnp.float32) * scale[g : g + 1, :]

    def group_rows(order):
        return 128 if order[0] == "z" else 112

    def load(p, order, block, c, g):
        if order[0] == "y":
            start = block * (8 * own * SIDE) + c * (4 * own * SIDE) + g * 112
            return total[p, pl.ds(pl.multiple_of(start, 8), 112), :]
        if order[0] == "x":
            starts = [(2 * g + n) * (8 * own * SIDE) + c * (4 * own * SIDE) + block * (own * SIDE) for n in range(2)]
            return jnp.concatenate([total[p, pl.ds(pl.multiple_of(s, 8), 56), :] for s in starts], axis=0)
        starts = [
            (2 * g + n) * (8 * own * SIDE) + c * (4 * own * SIDE) + m * (own * SIDE) + block * own
            for n in range(2) for m in range(SIDE)
        ]
        return jnp.concatenate([total[p, pl.ds(s, 16), :] for s in starts], axis=0)

    def second_block(p, order, j):
        if order[0] != "z" or order[1] == "y":
            n = 64 if order[0] == "z" else 56
            starts = [c * 4 * n + j * n for c in range(2)]
        else:
            n = 16
            starts = [c * 256 + m * 64 + j * n for c in range(2) for m in range(SIDE)]
        return jnp.concatenate([first_sum[p, pl.ds(pl.multiple_of(s, 8), n), :] for s in starts], axis=0)

    def copy(here, there, a, b, to):
        return pltpu.make_async_remote_copy(
            src_ref=here, dst_ref=there, send_sem=a, recv_sem=b, device_id=to, device_id_type=MESH,
        )

    def sized(order, groups):
        return pl.ds(0, HEAD + groups * group_rows(order))

    def copy_one(p, s):
        order = orders[p]
        run = sized(order, 2)
        return copy(out_one.at[p, s, run], in_one.at[p, s, run], one_send.at[p, s], one_recv.at[p, s],
                    device(order[0], (1, 3)[s]))

    def copy_two(p, s):
        order = orders[p]
        run = sized(order, 4)
        return copy(out_two.at[p, s, run], in_two.at[p, s, run], two_send.at[p, s], two_recv.at[p, s],
                    device(order[0], (1, 3)[s]))

    def copy_three(p, d):
        order = orders[p]
        run = sized(order, 1)
        return copy(out_three.at[p, d - 1, run], in_three.at[p, d - 1, run], three_send.at[p, d - 1],
                    three_recv.at[p, d - 1], device(order[1], d))

    def copy_four(p, d, flip):
        s = 2 * d + flip - 1
        return copy(out_four.at[p, s], in_four.at[p, s], four_send.at[p, s], four_recv.at[p, s],
                    device(orders[p][2], d, flip))

    def step_one(p):
        order = orders[p]
        block = place(order[0], 2)
        for s in range(2):
            put(out_one.at[p, s], [load(p, order, block, s, g) for g in range(2)])
            copy_one(p, s).start()

    def step_two(p):
        order = orders[p]
        n = group_rows(order)
        for s in range(2):
            copy_one(p, s).wait_recv()
            block = place(order[0], (1, 3)[s])
            scale = powers(in_one.at[p, s])
            values = []
            for c in range(2):
                for g in range(2):
                    value = load(p, order, block, c, g)
                    if c == s:
                        value = value + get(in_one.at[p, s], scale, g, n)
                    values.append(value)
            put(out_two.at[p, s], values)
            copy_two(p, s).start()

    def step_three(p):
        order = orders[p]
        n = group_rows(order)
        for s in range(2):
            copy_two(p, s).wait_recv()
        scales = [powers(in_two.at[p, s]) for s in range(2)]
        for c in range(2):
            for g in range(2):
                value = load(p, order, at[order[0]], c, g)
                for s in range(2):
                    value = value + get(in_two.at[p, s], scales[s], 2 * c + g, n)
                first_sum[p, (2 * c + g) * n : (2 * c + g + 1) * n, :] = value
        for d in range(1, SIDE):
            put(out_three.at[p, d - 1], [second_block(p, order, place(order[1], d))])
            copy_three(p, d).start()

    def last_rows(order, c, k):
        if order[0] == "z":
            return pl.ds(pl.multiple_of(c * 64 + k * 16, 8), 16)
        return pl.ds(c * 4 * own + k * own, 16)

    def step_four(p):
        order = orders[p]
        n = group_rows(order)
        value = second_block(p, order, at[order[1]])
        for d in range(1, SIDE):
            copy_three(p, d).wait_recv()
            ref = in_three.at[p, d - 1]
            value = value + get(ref, powers(ref), 0, n)
        second_sum[p, 0:n, :] = value
        rows = lax.broadcasted_iota(jnp.int32, (16, LANES), 0)
        for d in range(SIDE):
            for flip in range(2):
                if d or flip:
                    c = 1 - core if flip else core
                    value = second_sum[p, last_rows(order, c, place(order[2], d)), :]
                    top = jnp.max(jnp.where(rows < own, jnp.abs(value), 0.0), axis=0, keepdims=True)
                    power = exponent(top)
                    code = jnp.round(value * (jnp.exp2(-power) * TOP))
                    code = jnp.where(rows < own, code, power)
                    out_four[p, 2 * d + flip - 1] = code.astype(jnp.int32).astype(jnp.int16)
                    copy_four(p, d, flip).start()

    def step_five(p):
        order = orders[p]
        for flip in range(2):
            c = 1 - core if flip else core
            value = None
            if not flip:
                value = second_sum[p, last_rows(order, core, at[order[2]]), :]
            for d in range(SIDE):
                if d or flip:
                    copy_four(p, d, flip).wait_recv()
                    code = in_four[p, 2 * d + flip - 1].astype(jnp.int32).astype(jnp.float32)
                    term = code * (jnp.exp2(code[own : own + 1, :]) * (1.0 / TOP))
                    value = term if value is None else value + term
            columns = pl.ds(pl.multiple_of(c * half + p * LANES, LANES), LANES)
            out_ref[:, columns] = value[0:own, :]

    early = depth // LANES * LANES
    chunks = [list(range(p, min(p + 2, parts))) for p in range(0, parts, 2)]
    turn(0, early)
    for tiles in chunks:
        multiply(tiles, 0, early, True)
    done = early
    for n in range(pieces):
        pair[n].wait_recv()
        ready = (depth + (n + 1) * piece) // LANES * LANES
        if ready > done:
            turn(done, ready)
            done = ready
    for tiles in chunks:
        multiply(tiles, early, 2 * depth, False)
        for p in tiles:
            step_one(p)
    for p in range(parts):
        step_two(p)
    for p in range(parts):
        step_three(p)
    for p in range(parts):
        step_four(p)
    for p in range(parts):
        step_five(p)

    for n in range(pieces):
        pair[n].wait_send()
    for p in range(parts):
        for s in range(2):
            copy_one(p, s).wait_send()
            copy_two(p, s).wait_send()
        for d in range(SIDE):
            if d:
                copy_three(p, d).wait_send()
            for flip in range(2):
                if d or flip:
                    copy_four(p, d, flip).wait_send()


def solution(mesh):
    groups, members = mesh.shape["grp"], mesh.shape["mem"]

    def on_device(factors, screen):
        aux_rows, occ_count, basis = factors.shape
        depth = aux_rows * occ_count
        own = basis // (groups * members)
        parts = basis // 2 // LANES
        pieces = 4
        dma = pltpu.SemaphoreType.DMA
        vmem = pl.BlockSpec(memory_space=pltpu.VMEM)
        slots = 2 * SIDE - 1

        def codes(count, rows):
            return pltpu.VMEM((parts, count, rows, LANES), jnp.int16)

        return pl.pallas_call(
            functools.partial(kernel, members, occ_count // screen.shape[1], ORDERS, pieces),
            out_shape=jax.ShapeDtypeStruct((own, basis), jnp.float32),
            in_specs=[pl.BlockSpec(memory_space=pl.ANY), pl.BlockSpec(memory_space=pltpu.SMEM)],
            out_specs=vmem,
            scratch_shapes=[
                pltpu.VMEM((2 * depth, basis), jnp.bfloat16),
                pltpu.VMEM((basis, 2 * depth), jnp.bfloat16),
                pltpu.VMEM((parts, basis + 8, LANES), jnp.float32),
                pltpu.VMEM((parts, 512, LANES), jnp.float32),
                pltpu.VMEM((parts, 128, LANES), jnp.float32),
                codes(2, HEAD + 256), codes(2, HEAD + 256),
                codes(2, HEAD + 512), codes(2, HEAD + 512),
                codes(3, HEAD + 128), codes(3, HEAD + 128),
                codes(slots, 16), codes(slots, 16),
                dma((pieces,)), dma((pieces,)), dma((pieces,)),
                dma((parts, 2)), dma((parts, 2)),
                dma((parts, 2)), dma((parts, 2)),
                dma((parts, 3)), dma((parts, 3)),
                dma((parts, slots)), dma((parts, slots)),
            ],
            compiler_params=pltpu.CompilerParams(
                collective_id=0, has_side_effects=True, vmem_limit_bytes=60 * 1024 * 1024
            ),
        )(factors.reshape(depth, basis), screen)

    placed = (P(("grp", "mem"), None, None), P(("grp", "mem"), None))
    return jax.shard_map(
        on_device, mesh=mesh, in_specs=placed, out_specs=P(("grp", "mem"), None), check_vma=False
    )
```

time: 106 us -> 44 us (0.42)
  Pallas kernels: 86.9 us -> 42.3 us
  local copies, waits for them, and re-layouts: 19 us -> 1.55 us
    pallas_call x1, Pallas kernels: 86.9 us -> 42.3 us  [on_device(): pl.pallas_call(functools.partial(kernel, members, occ_count // screen.sha...]
    unnamed x1, local copies, waits for them, and re-layouts: 8.16 us -> 1.55 us
    reshape x3 -> x0, local copies, waits for them, and re-layouts: 5.01 us -> none  [the longest x1 2.67 us: on_device(): rows = rows.reshape(depth, basis)]
    another operation x1 -> x0, local copies, waits for them, and re-layouts: 3.73 us -> none  [on_device(): rows = rows.reshape(depth, devices, real_rows)]
    pad x1 -> x0, local copies, waits for them, and re-layouts: 2.07 us -> none  [on_device(): rows = jnp.pad(rows, ((0, 0), (0, 0), (0, own_rows - real_rows)))]
where the time goes in v1:
time: 44 us; the launch traced here: 43.9 us
  Pallas kernels  42.3 us (96%)
  local copies, waits for them, and re-layouts  1.55 us (4%)
    pallas_call x1, Pallas kernels, on_device(): pl.pallas_call(functools.partial(kernel, members, occ_count // screen.sha...  42.3 us
    unnamed x1, local copies, waits for them, and re-layouts  1.55 us

profile of v1, /device:TPU:1, one launch (start us, length us, event | category | flops | bytes accessed | tf_op | source)
XLA Modules:
  0.0 43.9 jit_solution(6960709465067006098)
XLA Ops:
  0.0 42.3 %shard_map.28 = f32[14,1792]{1,0:T(8,128)} custom-call(bf16[576,1792]{1,0:T(8,128)(2,1)} %bitcast.1, s32[1,18]{1,0:T(1,128)} %screen_ref.1), custom_call_target="tpu_custom_call" | custom-call | tf_op jit(solution)/shard_map/pallas_call | solution.py:332
  42.3 1.6 %copy.4 = f32[14,1792]{1,0:T(8,128)} copy(f32[14,1792]{1,0:T(8,128)} %shard_map.28) | data formatting | bytes 200704

commit v2 on v1

--- a/solution.py
+++ b/solution.py
@@ -12,7 +12,8 @@
 SIDE = 4
 HEAD = 16
 MESH = pl.DeviceIdType.MESH
-ORDERS = ("yxz", "zxy", "xyz", "yxz", "zxy", "xyz", "yxz")
+ORDERS = ("yzx", "zxy", "xyz", "yzx", "zxy", "xyz", "wvz")
+PIECES = (192, 256, 128)
 
 
 def kernel(
@@ -32,12 +33,20 @@
     at = {"y": lax.div(grp, 2), "c": lax.rem(grp, 2), "x": lax.div(mem, SIDE), "z": lax.rem(mem, SIDE)}
     core = at["c"]
 
+    at["w"] = (1 - core) * at["y"] + core * at["x"]
+    at["v"] = core * at["y"] + (1 - core) * at["x"]
+
     def place(axis, d):
         return lax.rem(at[axis] + d, SIDE)
 
     def device(axis, d, flip=0):
         there = dict(at)
-        if d:
+        if d and axis in "wv":
+            moved = place(axis, d)
+            on_y = 1 - core if axis == "w" else core
+            there["y"] = on_y * moved + (1 - on_y) * at["y"]
+            there["x"] = (1 - on_y) * moved + on_y * at["x"]
+        elif d:
             there[axis] = place(axis, d)
         if flip:
             there["c"] = 1 - core
@@ -54,10 +63,10 @@
     for other in peers:
         pl.semaphore_signal(barrier, inc=1, device_id=other, device_id_type=MESH)
 
-    piece = depth // pieces
+    starts = [sum(pieces[:n]) for n in range(len(pieces) + 1)]
     loads = []
-    for n in range(pieces):
-        rows = pl.ds(n * piece, piece)
+    for n in range(len(pieces)):
+        rows = pl.ds(starts[n], pieces[n])
         loads.append(pltpu.make_async_copy(x_ref.at[rows], both.at[rows], load_sem.at[n]))
         loads[-1].start()
 
@@ -66,6 +75,7 @@
         total[p, basis:total_rows, :] = jnp.zeros((total_rows - basis, LANES), jnp.float32)
         tail = second_sum.shape[1]
         second_sum[p, tail - 16 : tail, :] = jnp.zeros((16, LANES), jnp.float32)
+        first_sum[p, 448:464, :] = jnp.zeros((16, LANES), jnp.float32)
 
     def mask(j, carry):
         rows = pl.ds(pl.multiple_of(j * width, width), width)
@@ -75,15 +85,15 @@
 
     pair = []
     partner = device("x", 0, 1)
-    for n in range(pieces):
+    for n in range(len(pieces)):
         loads[n].wait()
-        lax.fori_loop(n * piece // width, (n + 1) * piece // width, mask, 0)
+        lax.fori_loop(starts[n] // width, starts[n + 1] // width, mask, 0)
         if n == 0:
             pl.semaphore_wait(barrier, len(peers))
         pair.append(
             pltpu.make_async_remote_copy(
-                src_ref=both.at[pl.ds(n * piece, piece)],
-                dst_ref=both.at[pl.ds(depth + n * piece, piece)],
+                src_ref=both.at[pl.ds(starts[n], pieces[n])],
+                dst_ref=both.at[pl.ds(depth + starts[n], pieces[n])],
                 send_sem=pair_send.at[n], recv_sem=pair_recv.at[n],
                 device_id=partner, device_id_type=MESH,
             )
@@ -142,8 +152,11 @@
         if order[0] == "y":
             start = block * (8 * own * SIDE) + c * (4 * own * SIDE) + g * 112
             return total[p, pl.ds(pl.multiple_of(start, 8), 112), :]
-        if order[0] == "x":
-            starts = [(2 * g + n) * (8 * own * SIDE) + c * (4 * own * SIDE) + block * (own * SIDE) for n in range(2)]
+        if order[0] in "xw":
+            near, far = own * SIDE, 8 * own * SIDE
+            if order[0] == "w":
+                near, far = core * near + (1 - core) * far, (1 - core) * near + core * far
+            starts = [(2 * g + n) * far + c * (4 * own * SIDE) + block * near for n in range(2)]
             return jnp.concatenate([total[p, pl.ds(pl.multiple_of(s, 8), 56), :] for s in starts], axis=0)
         starts = [
             (2 * g + n) * (8 * own * SIDE) + c * (4 * own * SIDE) + m * (own * SIDE) + block * own
@@ -152,6 +165,9 @@
         return jnp.concatenate([total[p, pl.ds(s, 16), :] for s in starts], axis=0)
 
     def second_block(p, order, j):
+        if order[1] == "z":
+            starts = [c * (4 * own * SIDE) + m * (own * SIDE) + j * own for c in range(2) for m in range(SIDE)]
+            return jnp.concatenate([first_sum[p, pl.ds(s, 16), :] for s in starts], axis=0)
         if order[0] != "z" or order[1] == "y":
             n = 64 if order[0] == "z" else 56
             starts = [c * 4 * n + j * n for c in range(2)]
@@ -180,9 +196,12 @@
         return copy(out_two.at[p, s, run], in_two.at[p, s, run], two_send.at[p, s], two_recv.at[p, s],
                     device(order[0], (1, 3)[s]))
 
+    def second_rows(order):
+        return 128 if "z" in order[:2] else 112
+
     def copy_three(p, d):
         order = orders[p]
-        run = sized(order, 1)
+        run = pl.ds(0, HEAD + second_rows(order))
         return copy(out_three.at[p, d - 1, run], in_three.at[p, d - 1, run], three_send.at[p, d - 1],
                     three_recv.at[p, d - 1], device(order[1], d))
 
@@ -232,13 +251,13 @@
             copy_three(p, d).start()
 
     def last_rows(order, c, k):
-        if order[0] == "z":
+        if "z" in order[:2]:
             return pl.ds(pl.multiple_of(c * 64 + k * 16, 8), 16)
         return pl.ds(c * 4 * own + k * own, 16)
 
     def step_four(p):
         order = orders[p]
-        n = group_rows(order)
+        n = second_rows(order)
         value = second_block(p, order, at[order[1]])
         for d in range(1, SIDE):
             copy_three(p, d).wait_recv()
@@ -274,20 +293,18 @@
             columns = pl.ds(pl.multiple_of(c * half + p * LANES, LANES), LANES)
             out_ref[:, columns] = value[0:own, :]
 
-    early = depth // LANES * LANES
-    chunks = [list(range(p, min(p + 2, parts))) for p in range(0, parts, 2)]
-    turn(0, early)
-    for tiles in chunks:
-        multiply(tiles, 0, early, True)
-    done = early
-    for n in range(pieces):
+    first, rest = [0, 1, 2], [[3, 4], [5, 6]]
+    edges = [depth // LANES * LANES] + [depth + start for start in starts[1:]]
+    turn(0, edges[0])
+    multiply(first, 0, edges[0], True)
+    for n in range(len(pieces)):
         pair[n].wait_recv()
-        ready = (depth + (n + 1) * piece) // LANES * LANES
-        if ready > done:
-            turn(done, ready)
-            done = ready
-    for tiles in chunks:
-        multiply(tiles, early, 2 * depth, False)
+        turn(edges[n], edges[n + 1])
+        multiply(first, edges[n], edges[n + 1], False)
+    for p in first:
+        step_one(p)
+    for tiles in rest:
+        multiply(tiles, 0, 2 * depth, True)
         for p in tiles:
             step_one(p)
     for p in range(parts):
@@ -299,7 +316,7 @@
     for p in range(parts):
         step_five(p)
 
-    for n in range(pieces):
+    for n in range(len(pieces)):
         pair[n].wait_send()
     for p in range(parts):
         for s in range(2):
@@ -321,7 +338,7 @@
         depth = aux_rows * occ_count
         own = basis // (groups * members)
         parts = basis // 2 // LANES
-        pieces = 4
+        pieces = PIECES
         dma = pltpu.SemaphoreType.DMA
         vmem = pl.BlockSpec(memory_space=pltpu.VMEM)
         slots = 2 * SIDE - 1
@@ -344,7 +361,7 @@
                 codes(2, HEAD + 512), codes(2, HEAD + 512),
                 codes(3, HEAD + 128), codes(3, HEAD + 128),
                 codes(slots, 16), codes(slots, 16),
-                dma((pieces,)), dma((pieces,)), dma((pieces,)),
+                dma((len(pieces),)), dma((len(pieces),)), dma((len(pieces),)),
                 dma((parts, 2)), dma((parts, 2)),
                 dma((parts, 2)), dma((parts, 2)),
                 dma((parts, 3)), dma((parts, 3)),

time: 44 us -> 41.9 us (0.952)
  Pallas kernels: 42.3 us -> 40.1 us
    pallas_call x1, Pallas kernels: 42.3 us -> 40.1 us  [on_device(): pl.pallas_call(functools.partial(kernel, members, occ_count // screen.sha...]
where the time goes in v2:
time: 41.9 us; the launch traced here: 41.7 us
  Pallas kernels  40.1 us (96%)
  local copies, waits for them, and re-layouts  1.55 us (4%)
    pallas_call x1, Pallas kernels, on_device(): pl.pallas_call(functools.partial(kernel, members, occ_count // screen.sha...  40.1 us
    unnamed x1, local copies, waits for them, and re-layouts  1.55 us

profile of v2, /device:TPU:1, one launch (start us, length us, event | category | flops | bytes accessed | tf_op | source)
XLA Modules:
  0.0 41.7 jit_solution(2755517330713840520)
XLA Ops:
  0.0 40.1 %shard_map.28 = f32[14,1792]{1,0:T(8,128)} custom-call(bf16[576,1792]{1,0:T(8,128)(2,1)} %bitcast.1, s32[1,18]{1,0:T(1,128)} %screen_ref.1), custom_call_target="tpu_custom_call" | custom-call | tf_op jit(solution)/shard_map/pallas_call | solution.py:349
  40.1 1.6 %copy.4 = f32[14,1792]{1,0:T(8,128)} copy(f32[14,1792]{1,0:T(8,128)} %shard_map.28) | data formatting | bytes 200704

commit v3 on v2

--- a/solution.py
+++ b/solution.py
@@ -14,15 +14,17 @@
 MESH = pl.DeviceIdType.MESH
 ORDERS = ("yzx", "zxy", "xyz", "yzx", "zxy", "xyz", "wvz")
 PIECES = (192, 256, 128)
+MERGED = (3, 4, 5, 6)
+PLANE = 2 * SIDE * SIDE - 1
 
 
 def kernel(
     members, width, orders, pieces,
-    x_ref, screen_ref, out_ref,
-    both, turned, total, first_sum, second_sum,
-    out_one, in_one, out_two, in_two, out_three, in_three, out_four, in_four,
-    load_sem, pair_send, pair_recv, one_send, one_recv, two_send, two_recv,
-    three_send, three_recv, four_send, four_recv,
+    x_ref, flags_ref, out_ref,
+    screen_ref, both, turned, total, first_sum, second_sum,
+    out_one, in_one, out_two, in_two, out_three, in_three, out_four, in_four, out_plane, in_plane,
+    flag_sem, load_sem, pair_send, pair_recv, one_send, one_recv, two_send, two_recv,
+    three_send, three_recv, four_send, four_recv, plane_send, plane_recv,
 ):
     depth, basis = x_ref.shape
     own = out_ref.shape[0]
@@ -40,14 +42,18 @@
         return lax.rem(at[axis] + d, SIDE)
 
     def device(axis, d, flip=0):
+        return moved([(axis, d)], flip)
+
+    def moved(moves, flip=0):
         there = dict(at)
-        if d and axis in "wv":
-            moved = place(axis, d)
-            on_y = 1 - core if axis == "w" else core
-            there["y"] = on_y * moved + (1 - on_y) * at["y"]
-            there["x"] = (1 - on_y) * moved + on_y * at["x"]
-        elif d:
-            there[axis] = place(axis, d)
+        for axis, d in moves:
+            if d and axis in "wv":
+                to = place(axis, d)
+                on_y = 1 - core if axis == "w" else core
+                there["y"] = on_y * to + (1 - on_y) * there["y"]
+                there["x"] = (1 - on_y) * to + on_y * there["x"]
+            elif d:
+                there[axis] = place(axis, d)
         if flip:
             there["c"] = 1 - core
         return (there["y"] * 2 + there["c"], there["x"] * SIDE + there["z"])
@@ -64,6 +70,8 @@
         pl.semaphore_signal(barrier, inc=1, device_id=other, device_id_type=MESH)
 
     starts = [sum(pieces[:n]) for n in range(len(pieces) + 1)]
+    flags = pltpu.make_async_copy(flags_ref, screen_ref, flag_sem)
+    flags.start()
     loads = []
     for n in range(len(pieces)):
         rows = pl.ds(starts[n], pieces[n])
@@ -85,6 +93,7 @@
 
     pair = []
     partner = device("x", 0, 1)
+    flags.wait()
     for n in range(len(pieces)):
         loads[n].wait()
         lax.fori_loop(starts[n] // width, starts[n + 1] // width, mask, 0)
@@ -190,10 +199,11 @@
         return copy(out_one.at[p, s, run], in_one.at[p, s, run], one_send.at[p, s], one_recv.at[p, s],
                     device(order[0], (1, 3)[s]))
 
-    def copy_two(p, s):
-        order = orders[p]
-        run = sized(order, 4)
-        return copy(out_two.at[p, s, run], in_two.at[p, s, run], two_send.at[p, s], two_recv.at[p, s],
+    def copy_two(p, s, late):
+        order = orders[p]
+        run = sized(order, 2)
+        n = 2 * s + late
+        return copy(out_two.at[p, n, run], in_two.at[p, n, run], two_send.at[p, n], two_recv.at[p, n],
                     device(order[0], (1, 3)[s]))
 
     def second_rows(order):
@@ -217,35 +227,97 @@
             put(out_one.at[p, s], [load(p, order, block, s, g) for g in range(2)])
             copy_one(p, s).start()
 
+    def step_solo(p):
+        order = orders[p]
+        for s in range(2):
+            block = place(order[0], (1, 3)[s])
+            put(out_two.at[p, 2 * s], [load(p, order, block, 1 - s, g) for g in range(2)])
+            copy_two(p, s, 0).start()
+
     def step_two(p):
         order = orders[p]
         n = group_rows(order)
         for s in range(2):
             copy_one(p, s).wait_recv()
             block = place(order[0], (1, 3)[s])
-            scale = powers(in_one.at[p, s])
-            values = []
-            for c in range(2):
-                for g in range(2):
-                    value = load(p, order, block, c, g)
-                    if c == s:
-                        value = value + get(in_one.at[p, s], scale, g, n)
-                    values.append(value)
-            put(out_two.at[p, s], values)
-            copy_two(p, s).start()
-
-    def step_three(p):
+            ref = in_one.at[p, s]
+            scale = powers(ref)
+            put(out_two.at[p, 2 * s + 1], [load(p, order, block, s, g) + get(ref, scale, g, n) for g in range(2)])
+            copy_two(p, s, 1).start()
+
+    def collect(p):
         order = orders[p]
         n = group_rows(order)
         for s in range(2):
-            copy_two(p, s).wait_recv()
-        scales = [powers(in_two.at[p, s]) for s in range(2)]
+            for late in range(2):
+                copy_two(p, s, late).wait_recv()
         for c in range(2):
+            refs = [in_two.at[p, 2 * s + (1 if c == s else 0)] for s in range(2)]
+            scales = [powers(ref) for ref in refs]
             for g in range(2):
                 value = load(p, order, at[order[0]], c, g)
-                for s in range(2):
-                    value = value + get(in_two.at[p, s], scales[s], 2 * c + g, n)
+                for ref, scale in zip(refs, scales):
+                    value = value + get(ref, scale, g, n)
                 first_sum[p, (2 * c + g) * n : (2 * c + g + 1) * n, :] = value
+
+    def plane_rows(order, c, u, v):
+        if order[0] == "z":
+            steps = {"y": SIDE * 16, "x": 16} if order[1] == "y" else {"x": 16, "y": SIDE * 16}
+            return pl.ds(pl.multiple_of(c * 256 + u * steps[order[1]] + v * steps[order[2]], 8), 16)
+        step = own if order[1] == "z" else own * SIDE
+        other = own * SIDE if order[1] == "z" else own
+        return pl.ds(c * (4 * own * SIDE) + u * step + v * other, 16)
+
+    def plane_slot(du, dv, flip):
+        return (du * SIDE + dv) * 2 + flip - 1
+
+    def step_plane(q):
+        p = merged[q]
+        order = orders[p]
+        collect(p)
+        row = lax.rem(lax.broadcasted_iota(jnp.int32, (SIDE * 16, LANES), 0), 16)
+        for du in range(SIDE):
+            u = place(order[1], du)
+            for flip in range(2):
+                c = 1 - core if flip else core
+                value = jnp.concatenate(
+                    [first_sum[p, plane_rows(order, c, u, place(order[2], dv)), :] for dv in range(SIDE)], axis=0
+                )
+                power = exponent(jnp.max(jnp.abs(value), axis=0, keepdims=True))
+                code = jnp.where(row == own, power, jnp.round(value * (jnp.exp2(-power) * TOP)))
+                code = code.astype(jnp.int32).astype(jnp.int16)
+                for dv in range(SIDE):
+                    if du or dv or flip:
+                        n = plane_slot(du, dv, flip)
+                        out_plane[q, n] = code[dv * 16 : (dv + 1) * 16, :]
+                        copy(out_plane.at[q, n], in_plane.at[q, n], plane_send.at[q], plane_recv.at[q],
+                             moved([(order[1], du), (order[2], dv)], flip)).start()
+
+    def wait_plane(q, sent):
+        whole = copy(out_plane.at[q], in_plane.at[q], plane_send.at[q], plane_recv.at[q], partner)
+        whole.wait_send() if sent else whole.wait_recv()
+
+    def end_plane(q):
+        p = merged[q]
+        order = orders[p]
+        wait_plane(q, False)
+        for flip in range(2):
+            c = 1 - core if flip else core
+            value = None
+            if not flip:
+                value = first_sum[p, plane_rows(order, core, at[order[1]], at[order[2]]), :]
+            for du in range(SIDE):
+                for dv in range(SIDE):
+                    if du or dv or flip:
+                        code = in_plane[q, plane_slot(du, dv, flip)].astype(jnp.int32).astype(jnp.float32)
+                        term = code * (jnp.exp2(code[own : own + 1, :]) * (1.0 / TOP))
+                        value = term if value is None else value + term
+            columns = pl.ds(pl.multiple_of(c * half + p * LANES, LANES), LANES)
+            out_ref[:, columns] = value[0:own, :]
+
+    def step_three(p):
+        order = orders[p]
+        collect(p)
         for d in range(1, SIDE):
             put(out_three.at[p, d - 1], [second_block(p, order, place(order[1], d))])
             copy_three(p, d).start()
@@ -293,7 +365,9 @@
             columns = pl.ds(pl.multiple_of(c * half + p * LANES, LANES), LANES)
             out_ref[:, columns] = value[0:own, :]
 
-    first, rest = [0, 1, 2], [[3, 4], [5, 6]]
+    first, rest = [0, 1, 2], [[3, 4, 5, 6]]
+    merged = MERGED
+    apart = [p for p in range(parts) if p not in merged]
     edges = [depth // LANES * LANES] + [depth + start for start in starts[1:]]
     turn(0, edges[0])
     multiply(first, 0, edges[0], True)
@@ -303,17 +377,27 @@
         multiply(first, edges[n], edges[n + 1], False)
     for p in first:
         step_one(p)
-    for tiles in rest:
-        multiply(tiles, 0, 2 * depth, True)
-        for p in tiles:
-            step_one(p)
-    for p in range(parts):
+    for p in first:
+        step_solo(p)
+    late = rest[0]
+    multiply(late, 0, 2 * depth, True)
+    for p in late:
+        step_one(p)
+    for p in first:
         step_two(p)
-    for p in range(parts):
-        step_three(p)
-    for p in range(parts):
+    for p in late:
+        step_solo(p)
+    for p in late:
+        step_two(p)
+    for p in first:
+        step_plane(merged.index(p)) if p in merged else step_three(p)
+    for p in late:
+        step_plane(merged.index(p)) if p in merged else step_three(p)
+    for p in apart:
         step_four(p)
-    for p in range(parts):
+    for q in range(len(merged)):
+        end_plane(q)
+    for p in apart:
         step_five(p)
 
     for n in range(len(pieces)):
@@ -321,7 +405,11 @@
     for p in range(parts):
         for s in range(2):
             copy_one(p, s).wait_send()
-            copy_two(p, s).wait_send()
+            for late in range(2):
+                copy_two(p, s, late).wait_send()
+    for q in range(len(merged)):
+        wait_plane(q, True)
+    for p in apart:
         for d in range(SIDE):
             if d:
                 copy_three(p, d).wait_send()
@@ -349,26 +437,30 @@
         return pl.pallas_call(
             functools.partial(kernel, members, occ_count // screen.shape[1], ORDERS, pieces),
             out_shape=jax.ShapeDtypeStruct((own, basis), jnp.float32),
-            in_specs=[pl.BlockSpec(memory_space=pl.ANY), pl.BlockSpec(memory_space=pltpu.SMEM)],
+            in_specs=[pl.BlockSpec(memory_space=pltpu.HBM)] * 2,
             out_specs=vmem,
             scratch_shapes=[
+                pltpu.SMEM(screen.shape, jnp.int32),
                 pltpu.VMEM((2 * depth, basis), jnp.bfloat16),
                 pltpu.VMEM((basis, 2 * depth), jnp.bfloat16),
                 pltpu.VMEM((parts, basis + 8, LANES), jnp.float32),
                 pltpu.VMEM((parts, 512, LANES), jnp.float32),
                 pltpu.VMEM((parts, 128, LANES), jnp.float32),
                 codes(2, HEAD + 256), codes(2, HEAD + 256),
-                codes(2, HEAD + 512), codes(2, HEAD + 512),
+                codes(4, HEAD + 256), codes(4, HEAD + 256),
                 codes(3, HEAD + 128), codes(3, HEAD + 128),
                 codes(slots, 16), codes(slots, 16),
-                dma((len(pieces),)), dma((len(pieces),)), dma((len(pieces),)),
+                pltpu.VMEM((len(MERGED), PLANE, 16, LANES), jnp.int16),
+                pltpu.VMEM((len(MERGED), PLANE, 16, LANES), jnp.int16),
+                dma, dma((len(pieces),)), dma((len(pieces),)), dma((len(pieces),)),
                 dma((parts, 2)), dma((parts, 2)),
-                dma((parts, 2)), dma((parts, 2)),
+                dma((parts, 4)), dma((parts, 4)),
                 dma((parts, 3)), dma((parts, 3)),
                 dma((parts, slots)), dma((parts, slots)),
+                dma((len(MERGED),)), dma((len(MERGED),)),
             ],
             compiler_params=pltpu.CompilerParams(
-                collective_id=0, has_side_effects=True, vmem_limit_bytes=60 * 1024 * 1024
+                collective_id=0, has_side_effects=True, vmem_limit_bytes=53 * 1024 * 1024
             ),
         )(factors.reshape(depth, basis), screen)
 

time: 41.9 us -> 38.2 us (0.912)
  Pallas kernels: 40.1 us -> 36.8 us
    pallas_call x1, Pallas kernels: 40.1 us -> 36.8 us  [on_device(): pl.pallas_call(functools.partial(kernel, members, occ_count // screen.sha...]
    unnamed x1 -> x3, local copies, waits for them, and re-layouts: 1.55 us -> 1.3 us
where the time goes in v3:
time: 38.2 us; the launch traced here: 38.1 us
  Pallas kernels  36.8 us (96%)
  local copies, waits for them, and re-layouts  1.3 us (3%)
    pallas_call x1, Pallas kernels, on_device(): pl.pallas_call(functools.partial(kernel, members, occ_count // screen.sha...  36.8 us
    unnamed x3, local copies, waits for them, and re-layouts  1.3 us

profile of v3, /device:TPU:1, one launch (start us, length us, event | category | flops | bytes accessed | tf_op | source)
XLA Modules:
  0.0 38.1 jit_solution(9722131435043054200)
XLA Ops:
  0.0 0.0 copy-start
  0.0 0.7 %copy-done = s32[1,18]{1,0:T(1,128)S(1)} copy-done((s32[1,18]{1,0:T(1,128)S(1)}, s32[1,18]{1,0:T(1,128)}, u32[]{:S(2)}) %copy-start) | copy-done | bytes 96
  0.7 36.8 %shard_map.28 = f32[14,1792]{1,0:T(8,128)S(1)} custom-call(bf16[576,1792]{1,0:T(8,128)(2,1)} %bitcast.1, s32[1,18]{1,0:T(1,128)S(1)} %copy-done), custom_call_target="tpu_custom_call" | custom-call | tf_op jit(solution)/shard_map/pallas_call | solution.py:437
  37.4 0.6 %copy.4 = f32[14,1792]{1,0:T(8,128)} copy(f32[14,1792]{1,0:T(8,128)S(1)} %shard_map.28) | data formatting | bytes 200704
Async XLA Ops:
  0.0 0.7 %copy-start = (s32[1,18]{1,0:T(1,128)S(1)}, s32[1,18]{1,0:T(1,128)}, u32[]{:S(2)}) copy-start(s32[1,18]{1,0:T(1,128)} %flags_ref.1) | copy-start | bytes 220

commit v4 on v3

--- a/solution.py
+++ b/solution.py
@@ -97,6 +97,7 @@
     for n in range(len(pieces)):
         loads[n].wait()
         lax.fori_loop(starts[n] // width, starts[n + 1] // width, mask, 0)
+    for n in range(len(pieces)):
         if n == 0:
             pl.semaphore_wait(barrier, len(peers))
         pair.append(
@@ -276,7 +277,7 @@
         order = orders[p]
         collect(p)
         row = lax.rem(lax.broadcasted_iota(jnp.int32, (SIDE * 16, LANES), 0), 16)
-        for du in range(SIDE):
+        for du in (2, 1, 3, 0):
             u = place(order[1], du)
             for flip in range(2):
                 c = 1 - core if flip else core
@@ -286,7 +287,7 @@
                 power = exponent(jnp.max(jnp.abs(value), axis=0, keepdims=True))
                 code = jnp.where(row == own, power, jnp.round(value * (jnp.exp2(-power) * TOP)))
                 code = code.astype(jnp.int32).astype(jnp.int16)
-                for dv in range(SIDE):
+                for dv in (2, 1, 3, 0):
                     if du or dv or flip:
                         n = plane_slot(du, dv, flip)
                         out_plane[q, n] = code[dv * 16 : (dv + 1) * 16, :]
@@ -371,10 +372,13 @@
     edges = [depth // LANES * LANES] + [depth + start for start in starts[1:]]
     turn(0, edges[0])
     multiply(first, 0, edges[0], True)
-    for n in range(len(pieces)):
+    pair[0].wait_recv()
+    turn(edges[0], edges[1])
+    multiply(first, edges[0], edges[1], False)
+    for n in range(1, len(pieces)):
         pair[n].wait_recv()
         turn(edges[n], edges[n + 1])
-        multiply(first, edges[n], edges[n + 1], False)
+    multiply(first, edges[1], 2 * depth, False)
     for p in first:
         step_one(p)
     for p in first:
@@ -385,14 +389,16 @@
         step_one(p)
     for p in first:
         step_two(p)
-    for p in late:
+    for p in late[:-1]:
         step_solo(p)
-    for p in late:
+    for p in late[:-1]:
         step_two(p)
+    step_solo(late[-1])
+    step_two(late[-1])
     for p in first:
-        step_plane(merged.index(p)) if p in merged else step_three(p)
-    for p in late:
-        step_plane(merged.index(p)) if p in merged else step_three(p)
+        step_three(p)
+    for q in (1, 0, 2, 3):
+        step_plane(q)
     for p in apart:
         step_four(p)
     for q in range(len(merged)):
@@ -462,7 +468,10 @@
             compiler_params=pltpu.CompilerParams(
                 collective_id=0, has_side_effects=True, vmem_limit_bytes=53 * 1024 * 1024
             ),
-        )(factors.reshape(depth, basis), screen)
+        )(
+            pltpu.with_memory_space_constraint(factors.reshape(depth, basis), pltpu.HBM),
+            pltpu.with_memory_space_constraint(screen, pltpu.HBM),
+        )
 
     placed = (P(("grp", "mem"), None, None), P(("grp", "mem"), None))
     return jax.shard_map(

time: 38.2 us -> 36.8 us (0.963)
  Pallas kernels: 36.8 us -> 36 us
  local copies, waits for them, and re-layouts: 1.3 us -> 0.65 us
    pallas_call x1, Pallas kernels: 36.8 us -> 36 us  [on_device(): pl.pallas_call(functools.partial(kernel, members, occ_count // screen.sha...]
    unnamed x3 -> x1, local copies, waits for them, and re-layouts: 1.3 us -> 0.65 us
where the time goes in v4:
time: 36.8 us; the launch traced here: 36.7 us
  Pallas kernels  36 us (98%)
  local copies, waits for them, and re-layouts  0.65 us (2%)
    pallas_call x1, Pallas kernels, on_device(): pl.pallas_call(functools.partial(kernel, members, occ_count // screen.sha...  36 us

profile of v4, /device:TPU:1, one launch (start us, length us, event | category | flops | bytes accessed | tf_op | source)
XLA Modules:
  0.0 36.7 jit_solution(4139856697695756617)
XLA Ops:
  0.0 36.0 %shard_map.28 = f32[14,1792]{1,0:T(8,128)S(1)} custom-call(bf16[576,1792]{1,0:T(8,128)(2,1)} %bitcast.1, s32[1,18]{1,0:T(1,128)} %flags_ref.1), custom_call_target="tpu_custom_call" | custom-call | tf_op jit(solution)/shard_map/pallas_call | solution.py:443
  36.0 0.6 %copy.4 = f32[14,1792]{1,0:T(8,128)} copy(f32[14,1792]{1,0:T(8,128)S(1)} %shard_map.28) | data formatting | bytes 200704

commit v5 on v4

--- a/solution.py
+++ b/solution.py
@@ -10,7 +10,7 @@
 LANES = 128
 TOP = 32767.0
 SIDE = 4
-HEAD = 16
+HEAD = 8
 MESH = pl.DeviceIdType.MESH
 ORDERS = ("yzx", "zxy", "xyz", "yzx", "zxy", "xyz", "wvz")
 PIECES = (192, 256, 128)
@@ -142,18 +142,19 @@
     def put(ref, values):
         rows = lax.broadcasted_iota(jnp.int32, (HEAD, LANES), 0)
         head = jnp.zeros((HEAD, LANES), jnp.float32)
+        end = sum(value.shape[0] for value in values)
         for g, value in enumerate(values):
             power = exponent(jnp.max(jnp.abs(value), axis=0, keepdims=True))
             n = value.shape[0]
-            ref[HEAD + g * n : HEAD + (g + 1) * n, :] = coded(value, power)
+            ref[g * n : (g + 1) * n, :] = coded(value, power)
             head = jnp.where(rows == g, power, head)
-        ref[0:HEAD, :] = head.astype(jnp.int32).astype(jnp.int16)
-
-    def powers(ref):
-        return jnp.exp2(ref[0:HEAD, :].astype(jnp.int32).astype(jnp.float32)) * (1.0 / TOP)
+        ref[end : end + HEAD, :] = head.astype(jnp.int32).astype(jnp.int16)
+
+    def powers(ref, end):
+        return jnp.exp2(ref[end : end + HEAD, :].astype(jnp.int32).astype(jnp.float32)) * (1.0 / TOP)
 
     def get(ref, scale, g, n):
-        return ref[HEAD + g * n : HEAD + (g + 1) * n, :].astype(jnp.int32).astype(jnp.float32) * scale[g : g + 1, :]
+        return ref[g * n : (g + 1) * n, :].astype(jnp.int32).astype(jnp.float32) * scale[g : g + 1, :]
 
     def group_rows(order):
         return 128 if order[0] == "z" else 112
@@ -242,7 +243,7 @@
             copy_one(p, s).wait_recv()
             block = place(order[0], (1, 3)[s])
             ref = in_one.at[p, s]
-            scale = powers(ref)
+            scale = powers(ref, 2 * n)
             put(out_two.at[p, 2 * s + 1], [load(p, order, block, s, g) + get(ref, scale, g, n) for g in range(2)])
             copy_two(p, s, 1).start()
 
@@ -254,7 +255,7 @@
                 copy_two(p, s, late).wait_recv()
         for c in range(2):
             refs = [in_two.at[p, 2 * s + (1 if c == s else 0)] for s in range(2)]
-            scales = [powers(ref) for ref in refs]
+            scales = [powers(ref, 2 * n) for ref in refs]
             for g in range(2):
                 value = load(p, order, at[order[0]], c, g)
                 for ref, scale in zip(refs, scales):
@@ -335,7 +336,7 @@
         for d in range(1, SIDE):
             copy_three(p, d).wait_recv()
             ref = in_three.at[p, d - 1]
-            value = value + get(ref, powers(ref), 0, n)
+            value = value + get(ref, powers(ref, n), 0, n)
         second_sum[p, 0:n, :] = value
         rows = lax.broadcasted_iota(jnp.int32, (16, LANES), 0)
         for d in range(SIDE):
@@ -401,24 +402,24 @@
         step_plane(q)
     for p in apart:
         step_four(p)
-    for q in range(len(merged)):
-        end_plane(q)
-    for p in apart:
-        step_five(p)
-
     for n in range(len(pieces)):
         pair[n].wait_send()
     for p in range(parts):
         for s in range(2):
             copy_one(p, s).wait_send()
-            for late in range(2):
-                copy_two(p, s, late).wait_send()
+            for late_half in range(2):
+                copy_two(p, s, late_half).wait_send()
+    for p in apart:
+        for d in range(1, SIDE):
+            copy_three(p, d).wait_send()
+    for q in (1, 0, 2, 3):
+        end_plane(q)
+    for p in apart:
+        step_five(p)
     for q in range(len(merged)):
         wait_plane(q, True)
     for p in apart:
         for d in range(SIDE):
-            if d:
-                copy_three(p, d).wait_send()
             for flip in range(2):
                 if d or flip:
                     copy_four(p, d, flip).wait_send()

time: 36.8 us -> 36.5 us (level)
  no operation moved by 1% of the time
where the time goes in v5:
time: 36.5 us; the launch traced here: 36.3 us
  Pallas kernels  35.7 us (98%)
  local copies, waits for them, and re-layouts  0.65 us (2%)
    pallas_call x1, Pallas kernels, on_device(): pl.pallas_call(functools.partial(kernel, members, occ_count // screen.sha...  35.7 us

profile of v5, /device:TPU:1, one launch (start us, length us, event | category | flops | bytes accessed | tf_op | source)
XLA Modules:
  0.0 36.3 jit_solution(17203699445423986374)
XLA Ops:
  0.0 35.7 %shard_map.28 = f32[14,1792]{1,0:T(8,128)S(1)} custom-call(bf16[576,1792]{1,0:T(8,128)(2,1)} %bitcast.1, s32[1,18]{1,0:T(1,128)} %flags_ref.1), custom_call_target="tpu_custom_call" | custom-call | tf_op jit(solution)/shard_map/pallas_call | solution.py:444
  35.7 0.6 %copy.4 = f32[14,1792]{1,0:T(8,128)} copy(f32[14,1792]{1,0:T(8,128)S(1)} %shard_map.28) | data formatting | bytes 200704

commit v6 on v5

--- a/solution.py
+++ b/solution.py
@@ -453,9 +453,9 @@
                 pltpu.VMEM((parts, basis + 8, LANES), jnp.float32),
                 pltpu.VMEM((parts, 512, LANES), jnp.float32),
                 pltpu.VMEM((parts, 128, LANES), jnp.float32),
-                codes(2, HEAD + 256), codes(2, HEAD + 256),
-                codes(4, HEAD + 256), codes(4, HEAD + 256),
-                codes(3, HEAD + 128), codes(3, HEAD + 128),
+                codes(2, 16 + 256), codes(2, 16 + 256),
+                codes(4, 16 + 256), codes(4, 16 + 256),
+                codes(3, 16 + 128), codes(3, 16 + 128),
                 codes(slots, 16), codes(slots, 16),
                 pltpu.VMEM((len(MERGED), PLANE, 16, LANES), jnp.int16),
                 pltpu.VMEM((len(MERGED), PLANE, 16, LANES), jnp.int16),

time: 36.5 us -> 36.5 us (level)
  no operation moved by 1% of the time
where the time goes in v6:
time: 36.5 us; the launch traced here: 36.3 us
  Pallas kernels  35.7 us (98%)
  local copies, waits for them, and re-layouts  0.65 us (2%)
    pallas_call x1, Pallas kernels, on_device(): pl.pallas_call(functools.partial(kernel, members, occ_count // screen.sha...  35.7 us

profile of v6, /device:TPU:1, one launch (start us, length us, event | category | flops | bytes accessed | tf_op | source)
XLA Modules:
  0.0 36.3 jit_solution(11378237196846615355)
XLA Ops:
  0.0 35.7 %shard_map.28 = f32[14,1792]{1,0:T(8,128)S(1)} custom-call(bf16[576,1792]{1,0:T(8,128)(2,1)} %bitcast.1, s32[1,18]{1,0:T(1,128)} %flags_ref.1), custom_call_target="tpu_custom_call" | custom-call | tf_op jit(solution)/shard_map/pallas_call | solution.py:444
  35.7 0.6 %copy.4 = f32[14,1792]{1,0:T(8,128)} copy(f32[14,1792]{1,0:T(8,128)S(1)} %shard_map.28) | data formatting | bytes 200704

commit v7 on v6

--- a/solution.py
+++ b/solution.py
@@ -88,7 +88,7 @@
     def mask(j, carry):
         rows = pl.ds(pl.multiple_of(j * width, width), width)
         keep = screen_ref[0, lax.rem(j, occ_blocks)].astype(jnp.float32)
-        both[rows, :] = (both[rows, :].astype(jnp.float32) * keep).astype(both.dtype)
+        both[rows, :] = both[rows, :] * jnp.full((width, basis), keep, jnp.float32).astype(both.dtype)
         return carry
 
     pair = []

time: 36.5 us -> 36.5 us (level)
  no operation moved by 1% of the time
where the time goes in v7:
time: 36.5 us; the launch traced here: 36.4 us
  Pallas kernels  35.7 us (98%)
  local copies, waits for them, and re-layouts  0.65 us (2%)
    pallas_call x1, Pallas kernels, on_device(): pl.pallas_call(functools.partial(kernel, members, occ_count // screen.sha...  35.7 us

profile of v7, /device:TPU:1, one launch (start us, length us, event | category | flops | bytes accessed | tf_op | source)
XLA Modules:
  0.0 36.4 jit_solution(10367878559082460543)
XLA Ops:
  0.0 35.7 %shard_map.28 = f32[14,1792]{1,0:T(8,128)S(1)} custom-call(bf16[576,1792]{1,0:T(8,128)(2,1)} %bitcast.1, s32[1,18]{1,0:T(1,128)} %flags_ref.1), custom_call_target="tpu_custom_call" | custom-call | tf_op jit(solution)/shard_map/pallas_call | solution.py:444
  35.7 0.6 %copy.4 = f32[14,1792]{1,0:T(8,128)} copy(f32[14,1792]{1,0:T(8,128)S(1)} %shard_map.28) | data formatting | bytes 200704

commit v8 on v6

--- a/solution.py
+++ b/solution.py
@@ -58,6 +58,15 @@
             there["c"] = 1 - core
         return (there["y"] * 2 + there["c"], there["x"] * SIDE + there["z"])
 
+    starts = [sum(pieces[:n]) for n in range(len(pieces) + 1)]
+    flags = pltpu.make_async_copy(flags_ref, screen_ref, flag_sem)
+    flags.start()
+    loads = []
+    for n in range(len(pieces)):
+        rows = pl.ds(starts[n], pieces[n])
+        loads.append(pltpu.make_async_copy(x_ref.at[rows], both.at[rows], load_sem.at[n]))
+        loads[-1].start()
+
     last_axes = sorted({order[2] for order in orders})
     peers = [device("x", 0, 1)]
     for axis in "xyz":
@@ -68,15 +77,6 @@
     barrier = pltpu.get_barrier_semaphore()
     for other in peers:
         pl.semaphore_signal(barrier, inc=1, device_id=other, device_id_type=MESH)
-
-    starts = [sum(pieces[:n]) for n in range(len(pieces) + 1)]
-    flags = pltpu.make_async_copy(flags_ref, screen_ref, flag_sem)
-    flags.start()
-    loads = []
-    for n in range(len(pieces)):
-        rows = pl.ds(starts[n], pieces[n])
-        loads.append(pltpu.make_async_copy(x_ref.at[rows], both.at[rows], load_sem.at[n]))
-        loads[-1].start()
 
     total_rows = total.shape[1]
     for p in range(parts):

time: 36.5 us -> 36.5 us (level)
  no operation moved by 1% of the time
where the time goes in v8:
time: 36.5 us; the launch traced here: 36.4 us
  Pallas kernels  35.7 us (98%)
  local copies, waits for them, and re-layouts  0.65 us (2%)
    pallas_call x1, Pallas kernels, on_device(): pl.pallas_call(functools.partial(kernel, members, occ_count // screen.sha...  35.7 us

profile of v8, /device:TPU:1, one launch (start us, length us, event | category | flops | bytes accessed | tf_op | source)
XLA Modules:
  0.0 36.4 jit_solution(673855427038714918)
XLA Ops:
  0.0 35.7 %shard_map.28 = f32[14,1792]{1,0:T(8,128)S(1)} custom-call(bf16[576,1792]{1,0:T(8,128)(2,1)} %bitcast.1, s32[1,18]{1,0:T(1,128)} %flags_ref.1), custom_call_target="tpu_custom_call" | custom-call | tf_op jit(solution)/shard_map/pallas_call | solution.py:444
  35.7 0.6 %copy.4 = f32[14,1792]{1,0:T(8,128)} copy(f32[14,1792]{1,0:T(8,128)S(1)} %shard_map.28) | data formatting | bytes 200704
